TPU v7x, 32 devices: a whole 2x2x4 slice. The times are simulated.
32 devices in a mesh: ia: 2 (over x), ja: 4 (over z), ka: 4 (over y, core).
Axes of the slice: x: 2, y: 2, z: 4, core: 2. Of those that a mesh axis runs over, the one named last changes fastest.
Arguments:
- tensor: bfloat16 [128, 256, 2, 512], P('ia', 'ja', None, 'ka'), may hold values from -6 to 6
- factor_two: float32 [256, 32], P('ja'), may hold values from -2 to 2
- factor_three: float32 [512, 32], P('ka'), may hold values from -2 to 2
- factor_four: float32 [2, 32], replicated, may hold values from -2 to 2
Outputs:
- new_one: float32 [128, 32], P('ia')
- new_two: float32 [256, 32], P('ja')
All inputs are finite; a program needn't handle non-finite values.
Results may differ from a plain program's by a relative error of at most 0.0042.
Values sent between devices are 32-bit elements; how exact they have to be, the bound alone decides.
A program may use at most 64 MiB of HBM per device.

v0:
```python
import jax
import jax.numpy as jnp
from jax import lax
from jax.sharding import PartitionSpec as P


def solve_rows(rhs, system):
    lower = jnp.linalg.cholesky(system)
    return jax.scipy.linalg.cho_solve((lower, True), rhs.T).T


def gram(factor):
    return jnp.dot(factor.T, factor, precision=lax.Precision.HIGHEST)


def along_two(root, factor):
    return jnp.einsum("abr,br->ar", root, factor, precision=lax.Precision.HIGHEST)


def along_one(root, factor):
    return jnp.einsum("abr,ar->br", root, factor, precision=lax.Precision.HIGHEST)


def per_device(tensor, factor_two, factor_three, factor_four):
    rows_first, rows_second, fourth_len, rows_third = tensor.shape
    rank_cols = factor_two.shape[1]
    khatri = (
        (factor_four[:, None, :] * factor_three[None, :, :])
        .reshape(fourth_len * rows_third, rank_cols)
        .astype(jnp.bfloat16)
    )
    local_root = jnp.dot(
        tensor.reshape(rows_first * rows_second, fourth_len * rows_third),
        khatri,
        preferred_element_type=jnp.float32,
    )
    gram_four = gram(factor_four)
    own_two = gram(factor_two)
    own_three = gram(factor_three)
    gram_two = lax.psum(own_two, "ja")
    gram_three = lax.psum(own_three, "ka")
    root = lax.psum(local_root.reshape(rows_first, rows_second * rank_cols), "ka")
    root = root.reshape(rows_first, rows_second, rank_cols)
    mode_one = lax.psum(along_two(root, factor_two), "ja")
    new_one = solve_rows(mode_one, gram_two * gram_three * gram_four)
    gram_one = lax.psum(gram(new_one), "ia")
    mode_two = lax.psum(along_one(root, new_one), "ia")
    new_two = solve_rows(mode_two, gram_one * gram_three * gram_four)
    return (new_one, new_two)


def solution(mesh):
    return jax.shard_map(
        per_device,
        mesh=mesh,
        in_specs=(P("ia", "ja", None, "ka"), P("ja", None), P("ka", None), P()),
        out_specs=(P("ia", None), P("ja", None)),
        check_vma=False,
    )
```

profile of v0, /device:TPU:0, one launch (start us, length us, event | category | flops | bytes accessed | tf_op | source)
XLA Modules:
  0.0 106.4 jit_solution(6343009016498718179)
XLA Ops:
  7.2 0.0 copy-start
  7.2 0.0 all-reduce.4.cloned.1.call-start
  7.2 0.8 copy.10
  8.0 0.7 multiply_convert_fusion
  8.7 0.0 copy-start.2
  8.8 2.3 %convolution_bitcast_fusion = f32[4096,32]{0,1:T(8,128)S(1)} fusion(bf16[256,32]{1,0:T(8,128)(2,1)S(1)} %bitcast.67, bf16[512,8,2,128]{3,2,1,0:T(2,128)(2,1)} %bitcast.64), kind=kOutput, calls=%fused_computation | convolution fusion | flops 67108864 | bytes 2637824 | tf_op jit(solution)/shard_map/dot_general | solution.py:32
  11.1 0.0 copy-start.3
  11.1 1.5 %reshape.40 = f32[64,64,32]{1,0,2:T(8,128)} reshape(f32[4096,32]{0,1:T(8,128)S(1)} %convolution_bitcast_fusion) | data formatting | bytes 1048576 | tf_op jit(solution)/shard_map/reshape | solution.py:43
  12.5 0.0 all-reduce.4.cloned.1.call-update
  12.6 0.0 copy-done.2
  12.6 0.1 fusion.14
  12.7 13.4 %psum.43 = f32[32,32]{0,1:T(8,128)S(1)} all-reduce(f32[32,32]{0,1:T(8,128)S(1)} %fusion.14), channel_id=1, replica_groups=mesh['ia'=2,'ja'=4,'ka'=4] {'ka'}, use_global_device_ids=true, to_apply=%region_1.0 | all-reduce | flops 1024 | bytes 8192 | tf_op jit(solution)/shard_map/psum | solution.py:41
  26.2 0.0 copy-done
  26.2 0.1 fusion.13
  26.3 25.4 %all-reduce.4.cloned.1.call-done = f32[64,64,32]{1,0,2:T(8,128)} async-done(((f32[64,64,32]{1,0,2:T(8,128)}), f32[64,64,32]{1,0,2:T(8,128)}) %all-reduce.4.cloned.1.call-update) | async-done | bytes 524304 | tf_op jit(solution)/shard_map/psum | solution.py:42
  51.8 3.0 %fusion.15 = f32[32,1,64]{2,1,0:T(1,128)S(1)} fusion(f32[64,64,32]{1,0,2:T(8,128)} %all-reduce.4.cloned.1.call-done, f32[64,32,1]{0,2,1:T(1,128)S(1)} %bitcast.63), kind=kOutput, calls=%fused_computation.30 | convolution fusion | flops 1572864 | bytes 540672 | tf_op jit(solution)/shard_map/abr,br->ar/dot_general | solution.py:17
  54.7 19.0 %all-reduce = (f32[32,64]{1,0:T(8,128)S(1)}, f32[32,32]{0,1:T(8,128)S(1)}) all-reduce(f32[32,64]{1,0:T(8,128)S(1)} %bitcast.69, f32[32,32]{0,1:T(8,128)S(1)} %fusion.13), channel_id=1, replica_groups=mesh['ia'=2,'ja'=4,'ka'=4] {'ja'}, use_global_device_ids=true, to_apply=%region_5.7 | all-reduce | flops 3072 | bytes 24576 | tf_op jit(solution)/shard_map/psum | solution.py:44
  73.7 0.0 copy-done.3
  73.7 0.2 multiply_multiply_fusion.1
  73.9 0.1 copy.9
  74.0 2.9 %cholesky.44 = f32[32,32]{1,0:T(8,128)S(1)} custom-call(f32[32,32]{1,0:T(8,128)S(1)} %fusion.12), custom_call_target="Cholesky" | custom-call | tf_op jit(solution)/shard_map/jit(cholesky)/cholesky | solution.py:8
  77.0 0.6 compare_reduce_fusion.1
  77.6 0.7 fusion.2
  78.3 2.4 %custom-call.8 = f32[1,32,32]{1,2,0:T(8,128)S(1)} custom-call(f32[1,32,32]{2,1,0:T(8,128)S(1)} %fusion.2), custom_call_target="InvertDiagBlocksLowerTriangular" | custom-call | tf_op jit(solution)/shard_map/jit(_cho_solve)/triangular_solve | solution.py:9
  80.7 0.2 fusion.10
  81.0 0.1 fusion.8
  81.1 0.0 copy-start.1
  81.1 0.2 fusion.16
  81.3 2.2 %fusion.17 = f32[32,1,64]{2,1,0:T(1,128)S(1)} fusion(f32[64,32,1]{0,2,1:T(1,128)S(1)} %bitcast.65, f32[64,64,32]{1,0,2:T(8,128)} %all-reduce.4.cloned.1.call-done), kind=kOutput, calls=%fused_computation.32 | convolution fusion | flops 1572864 | bytes 540672 | tf_op jit(solution)/shard_map/abr,ar->br/dot_general | solution.py:21
  83.4 8.3 %all-reduce.1 = (f32[32,64]{1,0:T(8,128)S(1)}, f32[32,32]{0,1:T(8,128)S(1)}) all-reduce(f32[32,64]{1,0:T(8,128)S(1)} %bitcast.68, f32[32,32]{0,1:T(8,128)S(1)} %fusion.16), channel_id=1, replica_groups=mesh['ia'=2,'ja'=4,'ka'=4] {'ia'}, use_global_device_ids=true, to_apply=%region_7.10 | all-reduce | flops 3072 | bytes 24576 | tf_op jit(solution)/shard_map/psum | solution.py:47
  91.8 0.1 copy.13
  91.9 2.9 %cholesky.55 = f32[32,32]{1,0:T(8,128)S(1)} custom-call(f32[32,32]{1,0:T(8,128)S(1)} %fusion.7), custom_call_target="Cholesky" | custom-call | tf_op jit(solution)/shard_map/jit(cholesky)/cholesky | solution.py:8
  94.8 0.6 compare_reduce_fusion
  95.5 0.7 fusion.3
  96.1 2.4 %custom-call.9 = f32[1,32,32]{1,2,0:T(8,128)S(1)} custom-call(f32[1,32,32]{2,1,0:T(8,128)S(1)} %fusion.3), custom_call_target="InvertDiagBlocksLowerTriangular" | custom-call | tf_op jit(solution)/shard_map/jit(_cho_solve)/triangular_solve | solution.py:9
  98.6 0.2 fusion.5
  98.8 0.8 convolution_bitcast_fusion.1
  99.5 0.0 copy-done.1
  (5 shorter events, 0.1 us)
Async XLA Ops:
  7.2 19.0 %copy-start = (f32[64,32]{0,1:T(8,128)S(1)}, f32[64,32]{0,1:T(8,128)}, u32[]{:S(2)}) copy-start(f32[64,32]{0,1:T(8,128)} %param.8) | copy-start | bytes 24580
  7.2 44.6 %all-reduce.4.cloned.1.call-start = ((), (), s32[]{:S(2)}) async-start(), calls=%async_computation | async-start | bytes 2097152 | tf_op jit(solution)/shard_map/psum | solution.py:42
  8.7 3.8 %copy-start.2 = (f32[128,32]{0,1:T(8,128)S(1)}, f32[128,32]{0,1:T(8,128)}, u32[]{:S(2)}) copy-start(f32[128,32]{0,1:T(8,128)} %param.9) | copy-start | bytes 49156
  11.1 62.6 %copy-start.3 = (f32[2,32]{1,0:T(2,128)S(1)}, f32[2,32]{1,0:T(2,128)}, u32[]{:S(2)}) copy-start(f32[2,32]{1,0:T(2,128)} %param.10) | copy-start | bytes 772
  81.1 18.5 %copy-start.1 = (f32[32,64]{1,0:T(8,128)}, f32[32,64]{1,0:T(8,128)S(1)}, u32[]{:S(2)}) copy-start(f32[32,64]{1,0:T(8,128)S(1)} %fusion.8) | copy-start | bytes 24580
Sparse Core Ops, SparseCore 0:
  12.7 39.0 all-reduce.3
where the time goes:
time: 107 us; the launch traced here: 106 us
  blocking collectives  40.8 us (38%)
  waiting for transfers between devices  25.4 us (24%)
  between operations  14.2 us (13%)
  other arithmetic  14.1 us (13%)
  matrix products  9.45 us (9%)
  local copies, waits for them, and re-layouts  2.46 us (2%)
    psum x1, waiting for transfers between devices, per_device(): lax.psum(local_root.reshape(rows_first, rows_second * rank_cols), 'ka')  25.4 us
    psum x1, blocking collectives, per_device(): mode_one = lax.psum(along_two(root, factor_two), 'ja')  19 us
    psum x1, blocking collectives, per_device(): gram_three = lax.psum(own_three, 'ka')  13.4 us
    psum x1, blocking collectives, per_device(): mode_two = lax.psum(along_one(root, new_one), 'ia')  8.31 us
    another operation x6, other arithmetic, solve_rows(): lower = jnp.linalg.cholesky(system)  7.19 us
    another operation x4, other arithmetic, solve_rows(): return jax.scipy.linalg.cho_solve((lower, True), rhs.T).T  6.17 us
    dot_general x1, matrix products, along_two(): jnp.einsum('abr,br->ar', root, factor, precision=lax.Precision.HIGHEST)  2.95 us
    dot_general x1, matrix products, per_device(): jnp.dot(tensor.reshape(rows_first * rows_second, fourth_len * rows_third)...  2.32 us
  transfers between devices with their start and end apart: 1, of which 1 were waited for; matrix products, arithmetic and copies ran while one was open for 0% of the time, Pallas kernels for 0%

commit v1 on v0

v1 whole, which is shorter than its diff:
```python
import functools

import jax
import jax.numpy as jnp
from jax import lax
from jax.experimental import pallas as pl
from jax.experimental.pallas import tpu as pltpu
from jax.sharding import PartitionSpec as P

MESH = pl.DeviceIdType.MESH
LANES = 128
SUBLANES = 8
EXACT = lax.Precision.HIGHEST


def dot_exact(left, right):
    return jnp.dot(left, right, precision=EXACT, preferred_element_type=jnp.float32)


def iota(shape, dim):
    return lax.broadcasted_iota(jnp.int32, shape, dim)


def spread(value, rank):
    return jnp.concatenate([value] * (LANES // rank), axis=1)


def pack(wide, rank):
    groups = LANES // rank
    rows = wide.shape[0] // groups
    group = iota((rows, LANES), 1) // rank
    packed = wide[:rows]
    for g in range(1, groups):
        packed = jnp.where(group == g, wide[g * rows:(g + 1) * rows], packed)
    return packed


def unpack_masked(packed, rank):
    group = iota(packed.shape, 1) // rank
    return jnp.concatenate(
        [jnp.where(group == g, packed, 0.0) for g in range(LANES // rank)], axis=0
    )


def inverse_wide(system_packed, rank):
    full = unpack_masked(system_packed, rank)
    shift = LANES // 2
    while shift >= rank:
        full = full + pltpu.roll(full, shift, 1)
        shift //= 2
    lane = iota((rank, LANES), 1)
    row = iota((rank, LANES), 0)
    work = jnp.where(lane < rank, full, jnp.where(lane % rank == row, 1.0, 0.0))
    for k in range(0, rank, 2):
        row_a, row_b = work[k:k + 1, :], work[k + 1:k + 2, :]
        col_a, col_b = work[:, k:k + 1], work[:, k + 1:k + 2]
        aa, ab = row_a[:, k:k + 1], row_a[:, k + 1:k + 2]
        ba, bb = row_b[:, k:k + 1], row_b[:, k + 1:k + 2]
        inv_a = 1.0 / aa
        ratio = ab * inv_a
        inv_b = 1.0 / (bb - ba * ratio)
        first = row_a * inv_a
        second = (row_b - ba * first) * inv_b
        first = first - ratio * second
        work = jnp.where(
            row == k, first, jnp.where(row == k + 1, second, work - col_a * first - col_b * second)
        )
    return jnp.where(lane < rank, pltpu.roll(work, rank, 1), work)


def kernel(
    sizes, chunks,
    tensor_hbm, two_hbm, three_hbm, four_hbm,
    one_out, two_out,
    slab, two_ref, three_ref, four_ref, root_ref, fold_ref,
    gram_two_slots, gram_three_slots, gram_one_slots, ka_slots, ja_slots, mix_slots,
    load_sems, small_sems,
    gram_two_send, gram_two_recv, gram_three_send, gram_three_recv,
    gram_one_send, gram_one_recv, ka_send, ka_recv, ja_send, ja_recv, mix_send, mix_recv,
):
    n_ia, n_ja, n_ka, rows_first, rows_second, fourth_len, rank = sizes
    halves = LANES // (fourth_len * rank)
    depth = rows_second * fourth_len
    half_first = rows_first // halves
    half_rows = half_first * depth
    per_chunk = half_first // chunks
    chunk_rows = per_chunk * depth
    my_ia, my_ja, my_ka = lax.axis_index("ia"), lax.axis_index("ja"), lax.axis_index("ka")

    small = [
        pltpu.make_async_copy(src, dst, small_sems.at[n])
        for n, (src, dst) in enumerate(
            ((two_hbm, two_ref), (three_hbm, three_ref), (four_hbm, four_ref))
        )
    ]
    for copy in small:
        copy.start()
    loads = []
    for c in range(chunks):
        for h in range(halves):
            part = pl.ds(h * half_rows + c * chunk_rows, chunk_rows)
            copy = pltpu.make_async_copy(
                tensor_hbm.at[part], slab.at[part], load_sems.at[c * halves + h]
            )
            copy.start()
            loads.append(copy)

    def mix_peer(d):
        place = lax.rem(my_ia * n_ka + my_ka + d, n_ia * n_ka)
        return place // n_ka, lax.rem(place, n_ka)

    barrier = pltpu.get_barrier_semaphore()
    for d in range(1, n_ja):
        pl.semaphore_signal(
            barrier, inc=1, device_id={"ja": lax.rem(my_ja + d, n_ja)}, device_id_type=MESH
        )
    for d in range(1, n_ia * n_ka):
        ia, ka = mix_peer(d)
        pl.semaphore_signal(
            barrier, inc=1, device_id={"ia": ia, "ka": ka}, device_id_type=MESH
        )

    def exchange(slots, send_sems, recv_sems, axis, me, count):
        copies = []
        for d in range(1, count):
            copy = pltpu.make_async_remote_copy(
                src_ref=slots.at[me], dst_ref=slots.at[me],
                send_sem=send_sems.at[d - 1], recv_sem=recv_sems.at[me],
                device_id={axis: lax.rem(me + d, count)}, device_id_type=MESH,
            )
            copy.start()
            copies.append(copy)
        return copies

    def gather(slots, send_sems, recv_sems, me, count):
        for d in range(1, count):
            source = lax.rem(me + d, count)
            pltpu.make_async_remote_copy(
                src_ref=slots.at[source], dst_ref=slots.at[source],
                send_sem=send_sems.at[d - 1], recv_sem=recv_sems.at[source],
                device_id={"ja": my_ja}, device_id_type=MESH,
            ).wait_recv()
        total = slots[0]
        for s in range(1, count):
            total = total + slots[s]
        return total

    for copy in small:
        copy.wait()
    two = spread(two_ref[...], rank)
    three = spread(three_ref[...], rank)
    four = four_ref[...]
    gram_two_slots[my_ja] = pack(dot_exact(two.T, two)[:rank], rank)
    gram_three_slots[my_ka] = pack(dot_exact(three.T, three)[:rank], rank)

    pl.semaphore_wait(barrier, n_ja - 1 + n_ia * n_ka - 1)
    pending = exchange(gram_two_slots, gram_two_send, gram_two_recv, "ja", my_ja, n_ja)
    pending += exchange(gram_three_slots, gram_three_send, gram_three_recv, "ka", my_ka, n_ka)

    four_wide = jnp.concatenate([four[l:l + 1] for l in range(fourth_len)] * halves, axis=1)
    khatri = three * four_wide
    lane_half = iota(khatri.shape, 1) // (fourth_len * rank)
    weights = jnp.concatenate(
        [jnp.where(lane_half == h, khatri, 0.0).astype(jnp.bfloat16) for h in range(halves)], axis=0
    )
    row_of = iota((depth, rows_second), 0) // fourth_len
    repeat_rows = jnp.where(row_of == iota((depth, rows_second), 1), 1.0, 0.0)
    lane_fourth = lax.rem(iota((depth, LANES), 1) // rank, fourth_len)
    own_fourth = lane_fourth == lax.rem(iota((depth, LANES), 0), fourth_len)
    scaled = jnp.where(own_fourth, dot_exact(repeat_rows, two), 0.0)

    sums = []
    for c in range(chunks):
        for h in range(halves):
            loads[c * halves + h].wait()
        left = jnp.concatenate(
            [slab[pl.ds(h * half_rows + c * chunk_rows, chunk_rows), :] for h in range(halves)], axis=1
        )
        block = jnp.dot(left, weights, preferred_element_type=jnp.float32)
        root_ref[pl.ds(c * chunk_rows, chunk_rows), :] = block
        for i in range(per_chunk):
            term = block[i * depth:(i + 1) * depth] * scaled
            sums.append(jnp.sum(term, axis=0, keepdims=True))
    mode = jnp.concatenate(sums, axis=0)
    step = rank
    lane = iota(mode.shape, 1)
    folded = mode
    for l in range(1, fourth_len):
        folded = folded + jnp.where(
            lax.rem(lane, fourth_len * rank) < (fourth_len - l) * rank,
            pltpu.roll(mode, LANES - l * rank, 1),
            pltpu.roll(mode, (fourth_len - l) * rank, 1),
        )
    sub_rows = half_first // fourth_len
    sub = lax.rem(iota((sub_rows, LANES), 1) // rank, fourth_len)
    packed = folded[:sub_rows]
    for l in range(1, fourth_len):
        packed = jnp.where(sub == l, folded[l * sub_rows:(l + 1) * sub_rows], packed)
    ka_slots[my_ka] = packed
    pending += exchange(ka_slots, ka_send, ka_recv, "ka", my_ka, n_ka)

    gram_three = gather(gram_three_slots, gram_three_send, gram_three_recv, my_ka, n_ka)
    own_four = pack(
        sum(four[l:l + 1].T * spread(four[l:l + 1], rank) for l in range(fourth_len)), rank
    )
    gram_fixed = gram_three * own_four

    ja_slots[my_ja] = gather(ka_slots, ka_send, ka_recv, my_ka, n_ka)
    pending += exchange(ja_slots, ja_send, ja_recv, "ja", my_ja, n_ja)

    gram_two = gather(gram_two_slots, gram_two_send, gram_two_recv, my_ja, n_ja)
    inv = inverse_wide(gram_two * gram_fixed, rank)
    inv = jnp.concatenate([inv] * (LANES // rank), axis=0)

    total = gather(ja_slots, ja_send, ja_recv, my_ja, n_ja)
    new_one = dot_exact(unpack_masked(total, rank), inv)
    gram_one_slots[my_ia] = pack(dot_exact(new_one.T, new_one)[:rank], rank)
    pending += exchange(gram_one_slots, gram_one_send, gram_one_recv, "ia", my_ia, n_ia)
    one_out[...] = new_one[:, :rank]

    half_of = iota((half_first, LANES), 1) // (fourth_len * rank)
    spread_one = new_one[:half_first]
    for h in range(1, halves):
        spread_one = jnp.where(half_of == h, new_one[h * half_first:(h + 1) * half_first], spread_one)
    acc = jnp.zeros((depth, LANES), jnp.float32)
    for i in range(half_first):
        acc = acc + root_ref[pl.ds(i * depth, depth), :] * spread_one[i:i + 1]
    acc = jnp.where(own_fourth, acc, 0.0)
    shift = LANES // 2
    while shift >= rank:
        acc = acc + pltpu.roll(acc, shift, 1)
        shift //= 2
    fold_ref[...] = acc
    mode_two = fold_ref[pl.ds(0, rows_second, fourth_len), :]
    for l in range(1, fourth_len):
        mode_two = mode_two + fold_ref[pl.ds(l, rows_second, fourth_len), :]
    my_mix = my_ia * n_ka + my_ka
    mix_slots[my_mix] = pack(mode_two, rank)
    for d in range(1, n_ia * n_ka):
        ia, ka = mix_peer(d)
        copy = pltpu.make_async_remote_copy(
            src_ref=mix_slots.at[my_mix], dst_ref=mix_slots.at[my_mix],
            send_sem=mix_send.at[d - 1], recv_sem=mix_recv.at[my_mix],
            device_id={"ia": ia, "ka": ka}, device_id_type=MESH,
        )
        copy.start()
        pending.append(copy)

    gram_one = gather(gram_one_slots, gram_one_send, gram_one_recv, my_ia, n_ia)
    inv = inverse_wide(gram_one * gram_fixed, rank)
    inv = jnp.concatenate([inv] * (LANES // rank), axis=0)
    total = gather(mix_slots, mix_send, mix_recv, my_mix, n_ia * n_ka)
    two_out[...] = dot_exact(unpack_masked(total, rank), inv)[:, :rank]

    for copy in pending:
        copy.wait_send()


def per_device(n_ia, n_ja, n_ka, tensor, factor_two, factor_three, factor_four):
    rows_first, rows_second, fourth_len, rows_third = tensor.shape
    rank = factor_two.shape[1]
    halves = LANES // (fourth_len * rank)
    depth = rows_second * fourth_len
    chunks = 4
    sizes = (n_ia, n_ja, n_ka, rows_first, rows_second, fourth_len, rank)
    gram_rows = rank * rank // LANES
    one_rows = rows_first * rank // LANES
    two_rows = rows_second * rank // LANES
    n_mix = n_ia * n_ka
    dma = pltpu.SemaphoreType.DMA

    def pair(count):
        return [dma((max(count - 1, 1),)), dma((count,))]

    f32 = jnp.float32
    return pl.pallas_call(
        functools.partial(kernel, sizes, chunks),
        out_shape=(
            jax.ShapeDtypeStruct((rows_first, rank), f32),
            jax.ShapeDtypeStruct((rows_second, rank), f32),
        ),
        in_specs=[pl.BlockSpec(memory_space=pl.ANY)] * 4,
        out_specs=(pl.BlockSpec(memory_space=pltpu.VMEM),) * 2,
        scratch_shapes=[
            pltpu.VMEM((rows_first * depth, rows_third), jnp.bfloat16),
            pltpu.VMEM(factor_two.shape, f32),
            pltpu.VMEM(factor_three.shape, f32),
            pltpu.VMEM(factor_four.shape, f32),
            pltpu.VMEM((rows_first * depth // halves, LANES), f32),
            pltpu.VMEM((depth, LANES), f32),
            pltpu.VMEM((n_ja, gram_rows, LANES), f32),
            pltpu.VMEM((n_ka, gram_rows, LANES), f32),
            pltpu.VMEM((n_ia, gram_rows, LANES), f32),
            pltpu.VMEM((n_ka, one_rows, LANES), f32),
            pltpu.VMEM((n_ja, one_rows, LANES), f32),
            pltpu.VMEM((n_mix, two_rows, LANES), f32),
            dma((chunks * halves,)),
            dma((3,)),
            *pair(n_ja), *pair(n_ka), *pair(n_ia), *pair(n_ka), *pair(n_ja), *pair(n_mix),
        ],
        compiler_params=pltpu.CompilerParams(collective_id=0, has_side_effects=True),
        name="als_sweep",
    )(
        tensor.reshape(rows_first * depth, rows_third), factor_two, factor_three, factor_four
    )


def solution(mesh):
    return jax.shard_map(
        functools.partial(per_device, mesh.shape["ia"], mesh.shape["ja"], mesh.shape["ka"]),
        mesh=mesh,
        in_specs=(P("ia", "ja", None, "ka"), P("ja", None), P("ka", None), P()),
        out_specs=(P("ia", None), P("ja", None)),
        check_vma=False,
    )
```

time: 107 us -> 32 us (0.30)
  blocking collectives: 40.8 us -> 0 us
  waiting for transfers between devices: 25.4 us -> 0 us
  Pallas kernels: 0 us -> 25.3 us
  other arithmetic: 14.1 us -> 0 us
  between operations: 14.2 us -> 0.64 us
  matrix products: 9.45 us -> 0 us
  local copies, waits for them, and re-layouts: 2.46 us -> 5.71 us
    psum x3 -> x0, blocking collectives: 40.8 us -> none  [the longest x1 19 us: per_device(): mode_one = lax.psum(along_two(root, factor_two), 'ja')]
    psum x1 -> x0, waiting for transfers between devices: 25.4 us -> none  [per_device(): lax.psum(local_root.reshape(rows_first, rows_second * rank_cols), 'ka')]
    pallas_call x0 -> x1, Pallas kernels: none -> 25.3 us  [per_device(): pl.pallas_call(functools.partial(kernel, sizes, chunks), out_shape=(jax.S...]
    another operation x10 -> x0, other arithmetic: 13.4 us -> none  [the longest x6 7.19 us: solve_rows(): lower = jnp.linalg.cholesky(system)]
    dot_general x7 -> x0, matrix products: 8.1 us -> none  [the longest x1 2.95 us: along_two(): jnp.einsum('abr,br->ar', root, factor, precision=lax.Precision.HIGHEST)]
    pallas_call x0 -> x2, local copies, waits for them, and re-layouts: none -> 2.87 us  [per_device(): pl.pallas_call(functools.partial(kernel, sizes, chunks), out_shape=(jax.S...]
    unnamed x9 -> x2, local copies, waits for them, and re-layouts: 0.85 us -> 2.84 us
    reshape x1 -> x0, local copies, waits for them, and re-layouts: 1.47 us -> none  [per_device(): root = root.reshape(rows_first, rows_second, rank_cols)]
  transfers between devices with their start and end apart: 1 -> 0, of which waited for: 1 -> 0; matrix products, arithmetic and copies ran while one was open for 0% -> 0% of each run, Pallas kernels for 0% -> 0%
where the time goes in v1:
time: 32 us; the launch traced here: 31.7 us
  Pallas kernels  25.3 us (79%)
  local copies, waits for them, and re-layouts  5.71 us (18%)
  between operations  0.64 us (2%)
    pallas_call x1, Pallas kernels, per_device(): pl.pallas_call(functools.partial(kernel, sizes, chunks), out_shape=(jax.S...  25.3 us
    pallas_call x2, local copies, waits for them, and re-layouts, per_device(): pl.pallas_call(functools.partial(kernel, sizes, chunks), out_shape=(jax.S...  2.87 us
    unnamed x2, local copies, waits for them, and re-layouts  2.84 us

profile of v1, /device:TPU:0, one launch (start us, length us, event | category | flops | bytes accessed | tf_op | source)
XLA Modules:
  0.0 31.7 jit_solution(12294835420754020850)
XLA Ops:
  0.6 1.4 %copy.6.two_hbm = f32[64,32]{1,0:T(8,128)} copy(f32[64,32]{0,1:T(8,128)} %param.5) | data formatting | bytes 16384 | tf_op args[1]
  2.0 1.4 %copy.7.three_hbm = f32[128,32]{1,0:T(8,128)} copy(f32[128,32]{0,1:T(8,128)} %param.6) | data formatting | bytes 32768 | tf_op args[2]
  3.5 25.3 %als_sweep.1 = (f32[64,32]{1,0:T(8,128)}, f32[64,32]{1,0:T(8,128)}) custom-call(bf16[8192,128]{1,0:T(8,128)(2,1)} %bitcast.1, f32[64,32]{1,0:T(8,128)} %copy.6.two_hbm, f32[128,32]{1,0:T(8,128)} %copy.7.three_hbm, f32[2,32]{1,0:T(2,128)} %four_hbm.1), custom_call_target="tpu_custom_call" | custom-call | tf_op jit(solution)/shard_map/als_sweep/pallas_call | solution.py:276
  28.8 1.4 %copy.8 = f32[64,32]{0,1:T(8,128)} copy(f32[64,32]{1,0:T(8,128)} %get-tuple-element.2) | data formatting | bytes 16384 | tf_op jit(solution)/shard_map/als_sweep/pallas_call | solution.py:276
  30.2 1.4 %copy.9 = f32[64,32]{0,1:T(8,128)} copy(f32[64,32]{1,0:T(8,128)} %get-tuple-element.3) | data formatting | bytes 16384 | tf_op jit(solution)/shard_map/als_sweep/pallas_call | solution.py:276

commit v2 on v1

--- a/solution.py
+++ b/solution.py
@@ -147,11 +147,12 @@
 
     for copy in small:
         copy.wait()
-    two = spread(two_ref[...], rank)
-    three = spread(three_ref[...], rank)
+    two_t, three_t = two_ref[...], three_ref[...]
+    two = jnp.concatenate([two_t] * (LANES // rank), axis=0).T
+    three = jnp.concatenate([three_t] * (LANES // rank), axis=0).T
     four = four_ref[...]
-    gram_two_slots[my_ja] = pack(dot_exact(two.T, two)[:rank], rank)
-    gram_three_slots[my_ka] = pack(dot_exact(three.T, three)[:rank], rank)
+    gram_two_slots[my_ja] = pack(dot_exact(two_t, two), rank)
+    gram_three_slots[my_ka] = pack(dot_exact(three_t, three), rank)
 
     pl.semaphore_wait(barrier, n_ja - 1 + n_ia * n_ka - 1)
     pending = exchange(gram_two_slots, gram_two_send, gram_two_recv, "ja", my_ja, n_ja)
@@ -214,9 +215,10 @@
 
     total = gather(ja_slots, ja_send, ja_recv, my_ja, n_ja)
     new_one = dot_exact(unpack_masked(total, rank), inv)
-    gram_one_slots[my_ia] = pack(dot_exact(new_one.T, new_one)[:rank], rank)
+    new_one_t = new_one.T[:rank]
+    gram_one_slots[my_ia] = pack(dot_exact(new_one_t, new_one), rank)
     pending += exchange(gram_one_slots, gram_one_send, gram_one_recv, "ia", my_ia, n_ia)
-    one_out[...] = new_one[:, :rank]
+    one_out[...] = new_one_t
 
     half_of = iota((half_first, LANES), 1) // (fourth_len * rank)
     spread_one = new_one[:half_first]
@@ -248,9 +250,11 @@
 
     gram_one = gather(gram_one_slots, gram_one_send, gram_one_recv, my_ia, n_ia)
     inv = inverse_wide(gram_one * gram_fixed, rank)
-    inv = jnp.concatenate([inv] * (LANES // rank), axis=0)
     total = gather(mix_slots, mix_send, mix_recv, my_mix, n_ia * n_ka)
-    two_out[...] = dot_exact(unpack_masked(total, rank), inv)[:, :rank]
+    two_out[...] = lax.dot_general(
+        inv, unpack_masked(total, rank), (((1,), (1,)), ((), ())),
+        precision=EXACT, preferred_element_type=jnp.float32,
+    )
 
     for copy in pending:
         copy.wait_send()
@@ -273,18 +277,18 @@
         return [dma((max(count - 1, 1),)), dma((count,))]
 
     f32 = jnp.float32
-    return pl.pallas_call(
+    one_t, two_t = pl.pallas_call(
         functools.partial(kernel, sizes, chunks),
         out_shape=(
-            jax.ShapeDtypeStruct((rows_first, rank), f32),
-            jax.ShapeDtypeStruct((rows_second, rank), f32),
+            jax.ShapeDtypeStruct((rank, rows_first), f32),
+            jax.ShapeDtypeStruct((rank, rows_second), f32),
         ),
         in_specs=[pl.BlockSpec(memory_space=pl.ANY)] * 4,
         out_specs=(pl.BlockSpec(memory_space=pltpu.VMEM),) * 2,
         scratch_shapes=[
             pltpu.VMEM((rows_first * depth, rows_third), jnp.bfloat16),
-            pltpu.VMEM(factor_two.shape, f32),
-            pltpu.VMEM(factor_three.shape, f32),
+            pltpu.VMEM(factor_two.shape[::-1], f32),
+            pltpu.VMEM(factor_three.shape[::-1], f32),
             pltpu.VMEM(factor_four.shape, f32),
             pltpu.VMEM((rows_first * depth // halves, LANES), f32),
             pltpu.VMEM((depth, LANES), f32),
@@ -301,8 +305,9 @@
         compiler_params=pltpu.CompilerParams(collective_id=0, has_side_effects=True),
         name="als_sweep",
     )(
-        tensor.reshape(rows_first * depth, rows_third), factor_two, factor_three, factor_four
-    )
+        tensor.reshape(rows_first * depth, rows_third), factor_two.T, factor_three.T, factor_four
+    )
+    return one_t.T, two_t.T
 
 
 def solution(mesh):

time: 32 us -> 29 us (0.906)
  local copies, waits for them, and re-layouts: 5.71 us -> 2.65 us
    pallas_call x2 -> x0, local copies, waits for them, and re-layouts: 2.87 us -> none  [per_device(): pl.pallas_call(functools.partial(kernel, sizes, chunks), out_shape=(jax.S...]
where the time goes in v2:
time: 29 us; the launch traced here: 28.6 us
  Pallas kernels  25.3 us (87%)
  local copies, waits for them, and re-layouts  2.65 us (9%)
  between operations  0.64 us (2%)
    pallas_call x1, Pallas kernels, per_device(): pl.pallas_call(functools.partial(kernel, sizes, chunks), out_shape=(jax.S...  25.3 us
    unnamed x2, local copies, waits for them, and re-layouts  2.65 us

profile of v2, /device:TPU:0, one launch (start us, length us, event | category | flops | bytes accessed | tf_op | source)
XLA Modules:
  0.0 28.6 jit_solution(9476220659470302524)
XLA Ops:
  0.6 25.3 %als_sweep.1 = (f32[32,64]{1,0:T(8,128)}, f32[32,64]{1,0:T(8,128)}) custom-call(bf16[8192,128]{1,0:T(8,128)(2,1)} %bitcast.5, f32[32,64]{1,0:T(8,128)} %bitcast.6, f32[32,128]{1,0:T(8,128)} %bitcast.7, f32[2,32]{1,0:T(2,128)} %four_hbm.1), custom_call_target="tpu_custom_call" | custom-call | tf_op jit(solution)/shard_map/als_sweep/pallas_call | solution.py:280
  26.0 1.3 %copy.8 = f32[64,32]{0,1:T(8,128)} copy(f32[64,32]{0,1:T(8,128)} %bitcast.9) | data formatting | bytes 16384
  27.3 1.3 %copy.9 = f32[64,32]{0,1:T(8,128)} copy(f32[64,32]{0,1:T(8,128)} %bitcast.8) | data formatting | bytes 16384

commit v3 on v2

--- a/solution.py
+++ b/solution.py
@@ -51,20 +51,34 @@
     lane = iota((rank, LANES), 1)
     row = iota((rank, LANES), 0)
     work = jnp.where(lane < rank, full, jnp.where(lane % rank == row, 1.0, 0.0))
-    for k in range(0, rank, 2):
-        row_a, row_b = work[k:k + 1, :], work[k + 1:k + 2, :]
-        col_a, col_b = work[:, k:k + 1], work[:, k + 1:k + 2]
-        aa, ab = row_a[:, k:k + 1], row_a[:, k + 1:k + 2]
-        ba, bb = row_b[:, k:k + 1], row_b[:, k + 1:k + 2]
-        inv_a = 1.0 / aa
-        ratio = ab * inv_a
-        inv_b = 1.0 / (bb - ba * ratio)
-        first = row_a * inv_a
-        second = (row_b - ba * first) * inv_b
-        first = first - ratio * second
-        work = jnp.where(
-            row == k, first, jnp.where(row == k + 1, second, work - col_a * first - col_b * second)
-        )
+    blocks = [work[b:b + SUBLANES] for b in range(0, rank, SUBLANES)]
+    sub = iota((SUBLANES, LANES), 0)
+
+    def eliminate(values, column, pivot_row, place):
+        out = [v - c * pivot_row for v, c in zip(values, column)]
+        home = place // SUBLANES
+        out[home] = jnp.where(sub == place % SUBLANES, pivot_row, out[home])
+        return out
+
+    def row_of(values, place):
+        at = place % SUBLANES
+        return values[place // SUBLANES][at:at + 1]
+
+    for start in range(0, rank, SUBLANES):
+        window = [
+            [jnp.broadcast_to(v[:, start + c:start + c + 1], (SUBLANES, LANES)) for v in blocks]
+            for c in range(SUBLANES)
+        ]
+        for c in range(SUBLANES):
+            place = start + c
+            column = window[c]
+            scale = 1.0 / row_of(column, place)
+            for later in range(c + 1, SUBLANES):
+                window[later] = eliminate(
+                    window[later], column, row_of(window[later], place) * scale, place
+                )
+            blocks = eliminate(blocks, column, row_of(blocks, place) * scale, place)
+    work = jnp.concatenate(blocks, axis=0)
     return jnp.where(lane < rank, pltpu.roll(work, rank, 1), work)
 
 
@@ -279,11 +293,8 @@
     f32 = jnp.float32
     one_t, two_t = pl.pallas_call(
         functools.partial(kernel, sizes, chunks),
-        out_shape=(
-            jax.ShapeDtypeStruct((rank, rows_first), f32),
-            jax.ShapeDtypeStruct((rank, rows_second), f32),
-        ),
-        in_specs=[pl.BlockSpec(memory_space=pl.ANY)] * 4,
+        out_shape=(pltpu.VMEM((rank, rows_first), f32), pltpu.VMEM((rank, rows_second), f32)),
+        in_specs=[pl.BlockSpec(memory_space=pltpu.HBM)] * 4,
         out_specs=(pl.BlockSpec(memory_space=pltpu.VMEM),) * 2,
         scratch_shapes=[
             pltpu.VMEM((rows_first * depth, rows_third), jnp.bfloat16),
@@ -307,6 +318,21 @@
     )(
         tensor.reshape(rows_first * depth, rows_third), factor_two.T, factor_three.T, factor_four
     )
+    def hand_on(one_ref, two_ref, one_out, two_out):
+        one_out[...] = one_ref[...]
+        two_out[...] = two_ref[...]
+
+    one_t, two_t = pl.pallas_call(
+        hand_on,
+        out_shape=(
+            jax.ShapeDtypeStruct((rank, rows_first), f32),
+            jax.ShapeDtypeStruct((rank, rows_second), f32),
+        ),
+        in_specs=[pl.BlockSpec(memory_space=pltpu.VMEM)] * 2,
+        out_specs=(pl.BlockSpec(memory_space=pltpu.VMEM),) * 2,
+        compiler_params=pltpu.CompilerParams(vmem_limit_bytes=2 * 1024 * 1024),
+        name="hand_on",
+    )(one_t, two_t)
     return one_t.T, two_t.T
 
 

time: 29 us -> 20.4 us (0.70)
  Pallas kernels: 25.3 us -> 19.6 us
  local copies, waits for them, and re-layouts: 2.65 us -> 0 us
    pallas_call x1 -> x2, Pallas kernels: 25.3 us -> 19.6 us  [the longest x1 19 us: per_device(): pl.pallas_call(functools.partial(kernel, sizes, chunks), out_shape=(pltpu...]
    unnamed x2 -> x0, local copies, waits for them, and re-layouts: 2.65 us -> none
where the time goes in v3:
time: 20.4 us; the launch traced here: 20.3 us
  Pallas kernels  19.6 us (96%)
  between operations  0.64 us (3%)
    pallas_call x1, Pallas kernels, per_device(): pl.pallas_call(functools.partial(kernel, sizes, chunks), out_shape=(pltpu...  19 us
    pallas_call x1, Pallas kernels, per_device(): pl.pallas_call(hand_on, out_shape=(jax.ShapeDtypeStruct((rank, rows_first...  0.61 us

profile of v3, /device:TPU:0, one launch (start us, length us, event | category | flops | bytes accessed | tf_op | source)
XLA Modules:
  0.0 20.3 jit_solution(11311933799688932793)
XLA Ops:
  0.6 19.0 %als_sweep.1 = (f32[32,64]{1,0:T(8,128)S(1)}, f32[32,64]{1,0:T(8,128)S(1)}) custom-call(bf16[8192,128]{1,0:T(8,128)(2,1)} %bitcast.5, f32[32,64]{1,0:T(8,128)} %bitcast.6, f32[32,128]{1,0:T(8,128)} %bitcast.7, f32[2,32]{1,0:T(2,128)} %four_hbm.1), custom_call_target="tpu_custom_call" | custom-call | tf_op jit(solution)/shard_map/als_sweep/pallas_call | solution.py:294
  19.7 0.6 %hand_on.1 = (f32[32,64]{1,0:T(8,128)}, f32[32,64]{1,0:T(8,128)}) custom-call(f32[32,64]{1,0:T(8,128)S(1)} %get-tuple-element.6.one_ref, f32[32,64]{1,0:T(8,128)S(1)} %get-tuple-element.7.two_ref), custom_call_target="tpu_custom_call" | custom-call | tf_op jit(solution)/shard_map/hand_on/pallas_call | solution.py:325

commit v4 on v3

--- a/solution.py
+++ b/solution.py
@@ -231,7 +231,10 @@
     new_one = dot_exact(unpack_masked(total, rank), inv)
     new_one_t = new_one.T[:rank]
     gram_one_slots[my_ia] = pack(dot_exact(new_one_t, new_one), rank)
-    pending += exchange(gram_one_slots, gram_one_send, gram_one_recv, "ia", my_ia, n_ia)
+    gram_copies = exchange(gram_one_slots, gram_one_send, gram_one_recv, "ia", my_ia, n_ia)
+    for copy in pending:
+        copy.wait_send()
+    pending = gram_copies
     one_out[...] = new_one_t
 
     half_of = iota((half_first, LANES), 1) // (fourth_len * rank)
@@ -279,7 +282,7 @@
     rank = factor_two.shape[1]
     halves = LANES // (fourth_len * rank)
     depth = rows_second * fourth_len
-    chunks = 4
+    chunks = 1
     sizes = (n_ia, n_ja, n_ka, rows_first, rows_second, fourth_len, rank)
     gram_rows = rank * rank // LANES
     one_rows = rows_first * rank // LANES

time: 20.4 us -> 19.3 us (0.946)
  Pallas kernels: 19.6 us -> 18.4 us
    pallas_call x1, Pallas kernels: 19 us -> 17.8 us  [per_device(): pl.pallas_call(functools.partial(kernel, sizes, chunks), out_shape=(pltpu...]
where the time goes in v4:
time: 19.3 us; the launch traced here: 19 us
  Pallas kernels  18.4 us (95%)
  between operations  0.64 us (3%)
    pallas_call x1, Pallas kernels, per_device(): pl.pallas_call(functools.partial(kernel, sizes, chunks), out_shape=(pltpu...  17.8 us
    pallas_call x1, Pallas kernels, per_device(): pl.pallas_call(hand_on, out_shape=(jax.ShapeDtypeStruct((rank, rows_first...  0.61 us

profile of v4, /device:TPU:0, one launch (start us, length us, event | category | flops | bytes accessed | tf_op | source)
XLA Modules:
  0.0 19.0 jit_solution(3218999689048112014)
XLA Ops:
  0.6 17.8 %als_sweep.1 = (f32[32,64]{1,0:T(8,128)S(1)}, f32[32,64]{1,0:T(8,128)S(1)}) custom-call(bf16[8192,128]{1,0:T(8,128)(2,1)} %bitcast.5, f32[32,64]{1,0:T(8,128)} %bitcast.6, f32[32,128]{1,0:T(8,128)} %bitcast.7, f32[2,32]{1,0:T(2,128)} %four_hbm.1), custom_call_target="tpu_custom_call" | custom-call | tf_op jit(solution)/shard_map/als_sweep/pallas_call | solution.py:297
  18.4 0.6 %hand_on.1 = (f32[32,64]{1,0:T(8,128)}, f32[32,64]{1,0:T(8,128)}) custom-call(f32[32,64]{1,0:T(8,128)S(1)} %get-tuple-element.6.one_ref, f32[32,64]{1,0:T(8,128)S(1)} %get-tuple-element.7.two_ref), custom_call_target="tpu_custom_call" | custom-call | tf_op jit(solution)/shard_map/hand_on/pallas_call | solution.py:328

commit v5 on v4

--- a/solution.py
+++ b/solution.py
@@ -64,20 +64,30 @@
         at = place % SUBLANES
         return values[place // SUBLANES][at:at + 1]
 
-    for start in range(0, rank, SUBLANES):
-        window = [
-            [jnp.broadcast_to(v[:, start + c:start + c + 1], (SUBLANES, LANES)) for v in blocks]
-            for c in range(SUBLANES)
+    span = 4
+
+    def spread_columns(start):
+        return [
+            [jnp.broadcast_to(v[:, at:at + 1], (SUBLANES, LANES)) for v in blocks]
+            for at in range(start, min(start + span, rank))
         ]
-        for c in range(SUBLANES):
+
+    window = spread_columns(0)
+    for start in range(0, rank, span):
+        ahead = spread_columns(start + span)
+        for c in range(span):
             place = start + c
             column = window[c]
             scale = 1.0 / row_of(column, place)
-            for later in range(c + 1, SUBLANES):
+            for later in range(c + 1, span):
                 window[later] = eliminate(
                     window[later], column, row_of(window[later], place) * scale, place
                 )
+            ahead = [
+                eliminate(values, column, row_of(values, place) * scale, place) for values in ahead
+            ]
             blocks = eliminate(blocks, column, row_of(blocks, place) * scale, place)
+        window = ahead
     work = jnp.concatenate(blocks, axis=0)
     return jnp.where(lane < rank, pltpu.roll(work, rank, 1), work)
 

time: 19.3 us -> 19.2 us (level)
  no operation moved by 1% of the time
where the time goes in v5:
time: 19.2 us; the launch traced here: 18.9 us
  Pallas kernels  18.3 us (95%)
  between operations  0.64 us (3%)
    pallas_call x1, Pallas kernels, per_device(): pl.pallas_call(functools.partial(kernel, sizes, chunks), out_shape=(pltpu...  17.7 us
    pallas_call x1, Pallas kernels, per_device(): pl.pallas_call(hand_on, out_shape=(jax.ShapeDtypeStruct((rank, rows_first...  0.61 us

profile of v5, /device:TPU:0, one launch (start us, length us, event | category | flops | bytes accessed | tf_op | source)
XLA Modules:
  0.0 18.9 jit_solution(17108887909560242812)
XLA Ops:
  0.6 17.7 %als_sweep.1 = (f32[32,64]{1,0:T(8,128)S(1)}, f32[32,64]{1,0:T(8,128)S(1)}) custom-call(bf16[8192,128]{1,0:T(8,128)(2,1)} %bitcast.5, f32[32,64]{1,0:T(8,128)} %bitcast.6, f32[32,128]{1,0:T(8,128)} %bitcast.7, f32[2,32]{1,0:T(2,128)} %four_hbm.1), custom_call_target="tpu_custom_call" | custom-call | tf_op jit(solution)/shard_map/als_sweep/pallas_call | solution.py:307
  18.3 0.6 %hand_on.1 = (f32[32,64]{1,0:T(8,128)}, f32[32,64]{1,0:T(8,128)}) custom-call(f32[32,64]{1,0:T(8,128)S(1)} %get-tuple-element.6.one_ref, f32[32,64]{1,0:T(8,128)S(1)} %get-tuple-element.7.two_ref), custom_call_target="tpu_custom_call" | custom-call | tf_op jit(solution)/shard_map/hand_on/pallas_call | solution.py:338
